TPU v7x, 32 devices: a whole 2x2x4 slice. The times are simulated.
32 devices in a mesh: wide: 8 (over y, x, core), narrow: 4 (over z).
Axes of the slice: x: 2, y: 2, z: 4, core: 2. Of those that a mesh axis runs over, the one named last changes fastest.
Arguments:
- measures: float32 [2, 48, 262144], P(None, 'narrow', 'wide'), may hold values from 0.1 to 10
- sku_brand: int32 [262144], P('wide'), may hold values from 0 to 8191, as said below
- sku_count: int32 [8], P('wide'), may hold values from 1024 to 32768, as said below
- brand_slot: int32 [8192], replicated, may hold values from 0 to 8191, as said below
- brand_category: int32 [8192], replicated, may hold values from 0 to 499
Outputs:
- brand_index: float32 [2, 48, 8192], P(None, 'narrow', 'wide')
- category_index: float32 [2, 48, 500], P(None, 'narrow')
Inputs may be any that keep to these rules, and one draw needn't show every extreme that they name: `sku_count`: the largest count is 32768 in every draw; the others are skewed below it. brand_slot is a permutation; columns k * 1024 to (k + 1) * 1024 - 1 form the k-th owner block. `sku_brand`: in every tile, slots o * 128 to (o + 1) * 128 - 1 name 128 distinct brands whose columns lie in owner block o, for every owner block o; every later slot of the tile names one of these brands; every brand is named by some live SKU.
All inputs are finite; a program needn't handle non-finite values.
Results may differ from a plain program's by a relative error of at most 0.002.
Values sent between devices are 32-bit elements; how exact they have to be, the bound alone decides.
A program may use at most 64 MiB of HBM per device.

v0:
```python
import math

import jax
import jax.numpy as jnp
from jax import lax
from jax.sharding import PartitionSpec as P

WEEKS = 48
CATS = 500
CAP = 128


def body(measures, sku_brand, sku_count, brand_slot, brand_category):
    kinds_here, weeks_local, tile_size = measures.shape
    measure_rows = kinds_here * weeks_local
    flat = measures.reshape(measure_rows, tile_size)
    wide_size = lax.axis_size("wide")
    brand_total = brand_slot.shape[0]
    owned_width = brand_total // wide_size
    list_count = wide_size * CAP
    live_count = sku_count[0]
    list_brands = sku_brand[:list_count]
    own_index = lax.axis_index("wide")
    own_columns = own_index * owned_width + jnp.arange(owned_width, dtype=jnp.int32)
    category_ids = jnp.arange(CATS, dtype=jnp.int32)
    brand_block = math.gcd(1024, brand_total)
    brand_trips = brand_total // brand_block

    def lookup(block_index, carry):
        list_columns, my_category, category_size = carry
        offset = block_index * brand_block
        block_slots = lax.dynamic_slice_in_dim(brand_slot, offset, brand_block, 0)
        block_cats = lax.dynamic_slice_in_dim(brand_category, offset, brand_block, 0)
        block_ids = offset + jnp.arange(brand_block, dtype=jnp.int32)
        list_columns = list_columns + jnp.sum(
            jnp.where(list_brands[:, None] == block_ids[None, :], block_slots[None, :], 0), axis=1
        )
        my_category = my_category + jnp.sum(
            jnp.where(own_columns[:, None] == block_slots[None, :], block_cats[None, :], 0), axis=1
        )
        category_size = category_size + jnp.sum(
            (block_cats[:, None] == category_ids[None, :]).astype(jnp.float32), axis=0
        )
        return (list_columns, my_category, category_size)

    start_lookup = (
        jnp.zeros((list_count,), jnp.int32),
        jnp.zeros((owned_width,), jnp.int32),
        jnp.zeros((CATS,), jnp.float32),
    )
    list_columns, my_category, category_size = lax.fori_loop(0, brand_trips, lookup, start_lookup)
    high_part = flat.astype(jnp.bfloat16)
    first_rest = flat - high_part.astype(jnp.float32)
    middle_part = first_rest.astype(jnp.bfloat16)
    low_part = (first_rest - middle_part.astype(jnp.float32)).astype(jnp.bfloat16)
    stacked = jnp.concatenate([high_part, middle_part, low_part], axis=0)
    block_size = math.gcd(2048, tile_size)
    block_trips = (live_count + block_size - 1) // block_size

    def accumulate(block_index, totals):
        offset = block_index * block_size
        values = lax.dynamic_slice_in_dim(stacked, offset, block_size, 1)
        target = lax.dynamic_slice_in_dim(sku_brand, offset, block_size, 0)
        is_live = offset + jnp.arange(block_size, dtype=jnp.int32) < live_count
        values = jnp.where(is_live[None, :], values, jnp.zeros((), jnp.bfloat16))
        member_table = (target[:, None] == list_brands[None, :]).astype(jnp.bfloat16)
        return totals + jnp.dot(values, member_table, preferred_element_type=jnp.float32)

    start_sums = jnp.zeros((3 * measure_rows, list_count), jnp.float32)
    summed = lax.fori_loop(0, block_trips, accumulate, start_sums)
    compact = (
        summed[:measure_rows] + summed[measure_rows : 2 * measure_rows] + summed[2 * measure_rows :]
    )
    local_labels = (list_columns % owned_width).reshape(wide_size, CAP)
    packed = compact.reshape(measure_rows, wide_size, CAP).transpose(1, 0, 2)
    labels = local_labels.astype(jnp.float32)
    arrived, arrived_ids = (
        lax.all_to_all(packed, "wide", split_axis=0, concat_axis=0, tiled=True),
        lax.all_to_all(labels, "wide", split_axis=0, concat_axis=0, tiled=True),
    )
    flat_ids = arrived_ids.reshape(-1).astype(jnp.int32)
    flat_values = arrived.transpose(1, 0, 2).reshape(measure_rows, -1)
    placing = (flat_ids[:, None] == jnp.arange(owned_width, dtype=jnp.int32)[None, :]).astype(
        jnp.float32
    )
    owned_sums = jnp.dot(
        flat_values, placing, precision=lax.Precision.HIGHEST, preferred_element_type=jnp.float32
    )
    membership = (my_category[:, None] == category_ids[None, :]).astype(jnp.float32)
    category_part = jnp.dot(
        owned_sums, membership, precision=lax.Precision.HIGHEST, preferred_element_type=jnp.float32
    )
    category_sums = lax.psum(category_part, "wide")
    brand_category_sum = jnp.dot(
        category_sums,
        membership.T,
        precision=lax.Precision.HIGHEST,
        preferred_element_type=jnp.float32,
    )
    brand_peers = jnp.dot(
        membership,
        category_size,
        precision=lax.Precision.HIGHEST,
        preferred_element_type=jnp.float32,
    )
    brand_index = owned_sums * brand_peers[None, :] / brand_category_sum
    by_kind = category_sums.reshape(kinds_here, weeks_local, CATS)
    kind_totals = jnp.sum(by_kind, axis=(1, 2))
    grand_sum = lax.psum(kind_totals, "narrow") / WEEKS
    category_index = by_kind * CATS / grand_sum[:, None, None]
    return (brand_index.reshape(kinds_here, weeks_local, owned_width), category_index)


def solution(mesh):
    placed = (P(None, "narrow", "wide"), P("wide"), P("wide"), P(), P())
    return jax.shard_map(
        body,
        mesh=mesh,
        in_specs=placed,
        out_specs=(P(None, "narrow", "wide"), P(None, "narrow", None)),
        check_vma=False,
    )
```

profile of v0, /device:TPU:0, one launch (start us, length us, event | category | flops | bytes accessed | tf_op | source)
XLA Modules:
  0.0 159.8 jit_solution(1127724570599743675)
XLA Ops:
  1.4 23.3 %while.29 = (s32[]{:T(128)}, s32[1024]{0:T(1024)S(1)}, s32[1024]{0:T(1024)S(1)}, f32[500]{0:T(512)S(1)}, s32[1024]{0:T(1024)S(1)}, /*index=5*/s32[8192]{0:T(1024...) while((s32[]{:T(128)}, s32[1024]{0:T(1024)S(1)}, ...), condition=%wide.region_6.7_spmd.clone, body=%wide.region_2.6_spmd.clone.sunk | while | flops 7832059 | bytes 90110 | solution.py:51
  2.7 1.2 select_reduce_fusion.3
  4.3 0.7 dynamic_slice.32
  5.7 1.2 select_reduce_fusion.3
  8.6 1.2 select_reduce_fusion.3
  11.5 1.2 select_reduce_fusion.3
  14.4 1.2 select_reduce_fusion.3
  17.3 1.2 select_reduce_fusion.3
  18.8 0.7 dynamic_slice.32
  20.2 1.2 select_reduce_fusion.3
  23.2 1.2 select_reduce_fusion.3
  25.3 5.2 %all-to-all-start.1 = ((f32[8,1,128]{2,1,0:T(1,128)}), f32[8,1,128]{2,1,0:T(1,128)S(1)}, u32[]{:S(2)}, u32[]{:S(2)}) async-start(f32[8,1,128]{2,1,0:T(1,128)} %bitcast.3), calls=%async_computation.1 | async-start | bytes 8192 | tf_op jit(solution)/shard_map/all_to_all | solution.py:79
  31.1 5.6 %copy.21 = f32[2,12,32768]{2,1,0:T(8,128)} copy(f32[2,12,32768]{2,0,1:T(2,128)} %param.9) | data formatting | bytes 6291456 | tf_op args[0]
  36.8 2.6 %reshape.62 = f32[24,32768]{1,0:T(8,128)S(1)} reshape(f32[2,12,32768]{2,1,0:T(8,128)} %copy.21) | data formatting | bytes 6291456 | tf_op jit(solution)/shard_map/reshape | solution.py:16
  39.3 2.5 %fusion.31 = (bf16[24,32768]{1,0:T(8,128)(2,1)}, bf16[24,32768]{1,0:T(8,128)(2,1)}, bf16[24,32768]{1,0:T(8,128)(2,1)}) fusion(f32[24,32768]{1,0:T(8,128)S(1)} %reshape.62), kind=kLoop, calls=%fused_computation.49 | loop fusion | flops 5505024 | bytes 7864320 | tf_op jit(solution)/shard_map/convert_element_type | solution.py:52
  41.8 3.9 %pad_maximum_fusion = bf16[72,32768]{1,0:T(8,128)(2,1)} fusion(bf16[24,32768]{1,0:T(8,128)(2,1)} %get-tuple-element.277, bf16[24,32768]{1,0:T(8,128)(2,1)} %get-tuple-element.278, bf16[24,32768]{1,0:T(8,128)(2,1)} %get-tuple-element.276), kind=kLoop, calls=%fused_computation.23 | loop fusion | flops 14155776 | bytes 9437184 | tf_op jit(solution)/shard_map/concatenate | solution.py:56
  45.7 12.0 %while.28 = (s32[]{:T(128)}, f32[72,1024]{1,0:T(8,128)S(1)}, s32[]{:T(128)}, s32[]{:T(128)}, bf16[72,32768]{1,0:T(8,128)(2,1)}, /*index=5*/s32[32768]{0:T(1024)}...) while((s32[]{:T(128)}, f32[72,1024]{1,0:T(8,128)S(1)}, s32[]{:T(128)}, ...), condition=%wide.region_1.0_spmd, body=%wide.region_0.1_spmd.sunk | while | flops 304312320 | bytes 917675 | solution.py:70
  45.8 0.7 dynamic_slice.31
  47.1 2.6 %fusion.42 = f32[72,1024]{1,0:T(8,128)S(1)} fusion(f32[72,1024]{1,0:T(8,128)S(1)} %get-tuple-element.430, s32[1024]{0:T(1024)S(1)} %get-tuple-element.446, s32[2048]{0:T(1024)S(1)} %dynamic_slice.31, bf16[72,32768]{1,0:T(8,128)(2,1)} %get-tuple-element.444, s32[]{:T(128)S(6)} %select_n.59, pred[2048]{0:T(1024)(128)(4,1)S(1)} %add_compare_fusion.2), kind=kOutput, calls=%fused_computation.6.clone.1 | convolution fusion | flops 304308224 | bytes 899076 | tf_op jit(solution)/shard_map/while/body/dot_general | solution.py:67
  49.8 0.7 dynamic_slice.31
  51.1 2.6 %fusion.42 = f32[72,1024]{1,0:T(8,128)S(1)} fusion(f32[72,1024]{1,0:T(8,128)S(1)} %get-tuple-element.430, s32[1024]{0:T(1024)S(1)} %get-tuple-element.446, s32[2048]{0:T(1024)S(1)} %dynamic_slice.31, bf16[72,32768]{1,0:T(8,128)(2,1)} %get-tuple-element.444, s32[]{:T(128)S(6)} %select_n.59, pred[2048]{0:T(1024)(128)(4,1)S(1)} %add_compare_fusion.2), kind=kOutput, calls=%fused_computation.6.clone.1 | convolution fusion | flops 304308224 | bytes 899076 | tf_op jit(solution)/shard_map/while/body/dot_general | solution.py:67
  53.8 0.7 dynamic_slice.31
  55.2 2.6 %fusion.42 = f32[72,1024]{1,0:T(8,128)S(1)} fusion(f32[72,1024]{1,0:T(8,128)S(1)} %get-tuple-element.430, s32[1024]{0:T(1024)S(1)} %get-tuple-element.446, s32[2048]{0:T(1024)S(1)} %dynamic_slice.31, bf16[72,32768]{1,0:T(8,128)(2,1)} %get-tuple-element.444, s32[]{:T(128)S(6)} %select_n.59, pred[2048]{0:T(1024)(128)(4,1)S(1)} %add_compare_fusion.2), kind=kOutput, calls=%fused_computation.6.clone.1 | convolution fusion | flops 304308224 | bytes 899076 | tf_op jit(solution)/shard_map/while/body/dot_general | solution.py:67
  58.5 56.1 %all-to-all-start = ((f32[8,24,128]{2,1,0:T(8,128)}), f32[8,24,128]{2,1,0:T(8,128)S(1)}, u32[]{:S(2)}, u32[]{:S(2)}) async-start(f32[8,24,128]{2,1,0:T(8,128)} %copy.22), calls=%async_computation | async-start | bytes 196608 | tf_op jit(solution)/shard_map/all_to_all | solution.py:78
  114.6 1.1 fusion.21
  115.7 4.1 %all-to-all-done = f32[8,24,128]{2,1,0:T(8,128)S(1)} async-done(((f32[8,24,128]{2,1,0:T(8,128)}), f32[8,24,128]{2,1,0:T(8,128)S(1)}, u32[]{:S(2)}, u32[]{:S(2)}) %all-to-all-start) | async-done | bytes 98336 | tf_op jit(solution)/shard_map/all_to_all | solution.py:78
  119.8 1.5 fusion.17
  121.3 0.8 fusion.20
  122.1 22.8 %psum.14 = f32[24,500]{1,0:T(8,128)S(1)} all-reduce(f32[24,500]{1,0:T(8,128)S(1)} %fusion.20), channel_id=1, replica_groups=mesh['wide'=8,'narrow'=4] {'wide'}, use_global_device_ids=true, to_apply=%region_7.8 | all-reduce | flops 12000 | bytes 96000 | tf_op jit(solution)/shard_map/psum | solution.py:93
  145.2 12.0 %psum.15 = f32[2]{0:T(128)S(1)} all-reduce(f32[2]{0:T(128)S(1)} %reduce_sum.57), channel_id=1, replica_groups=mesh['wide'=8,'narrow'=4] {'narrow'}, use_global_device_ids=true, to_apply=%region_10.11 | all-reduce | flops 2 | bytes 16 | tf_op jit(solution)/shard_map/psum | solution.py:109
  157.9 1.1 fusion.23
  159.1 0.7 copy.24
  (76 shorter events, 17.2 us)
Async XLA Ops:
  25.3 33.2 %all-to-all-start.1 = ((f32[8,1,128]{2,1,0:T(1,128)}), f32[8,1,128]{2,1,0:T(1,128)S(1)}, u32[]{:S(2)}, u32[]{:S(2)}) async-start(f32[8,1,128]{2,1,0:T(1,128)} %bitcast.3), calls=%async_computation.1 | async-start | bytes 8192 | tf_op jit(solution)/shard_map/all_to_all | solution.py:79
  58.5 61.3 %all-to-all-start = ((f32[8,24,128]{2,1,0:T(8,128)}), f32[8,24,128]{2,1,0:T(8,128)S(1)}, u32[]{:S(2)}, u32[]{:S(2)}) async-start(f32[8,24,128]{2,1,0:T(8,128)} %copy.22), calls=%async_computation | async-start | bytes 196608 | tf_op jit(solution)/shard_map/all_to_all | solution.py:78
where the time goes:
time: 161 us; the launch traced here: 160 us
  starting transfers between devices  61.3 us (38%)
  blocking collectives  34.7 us (22%)
  local copies, waits for them, and re-layouts  24.2 us (15%)
  other arithmetic  21.2 us (13%)
  matrix products  12.4 us (8%)
  waiting for transfers between devices  4.08 us (3%)
    all_to_all x1, starting transfers between devices, body(): lax.all_to_all(packed, 'wide', split_axis=0, concat_axis=0, tiled=True)  56.1 us
    psum x1, blocking collectives, body(): category_sums = lax.psum(category_part, 'wide')  22.8 us
    psum x1, blocking collectives, body(): grand_sum = lax.psum(kind_totals, 'narrow') / WEEKS  12 us
    reduce_sum x8, other arithmetic, lookup(): jnp.sum(jnp.where(own_columns[:, None] == block_slots[None, :], block_cat...  9.44 us
    dot_general x3, matrix products, accumulate(): jnp.dot(values, member_table, preferred_element_type=jnp.float32)  7.87 us
    unnamed x4, local copies, waits for them, and re-layouts  7.04 us
    dynamic_slice x8, local copies, waits for them, and re-layouts, lookup(): lax.dynamic_slice_in_dim(brand_category, offset, brand_block, 0)  5.54 us
    dynamic_slice x8, local copies, waits for them, and re-layouts, lookup(): block_slots = lax.dynamic_slice_in_dim(brand_slot, offset, brand_block, 0)  5.5 us
  transfers between devices with their start and end apart: 2, of which 1 were waited for; matrix products, arithmetic and copies ran while one was open for 18% of the time, Pallas kernels for 0%

commit v1 on v0

v1 whole, which is shorter than its diff:
```python
import functools

import jax
import jax.numpy as jnp
from jax import lax
from jax.experimental import pallas as pl
from jax.experimental.pallas import tpu as pltpu
from jax.sharding import PartitionSpec as P

CATS = 500
CAP = 128
LANES = 128
LOW = 256
CAT_BLOCKS = 4
CAT_PAD = CAT_BLOCKS * LANES
NT = (((1,), (1,)), ((), ()))
MESH = pl.DeviceIdType.MESH
F32 = jnp.float32
BF16 = jnp.bfloat16


def dot_nt(a, b):
    return lax.dot_general(a, b, NT, preferred_element_type=F32)


def rows_of(shape):
    return lax.broadcasted_iota(jnp.int32, shape, 0)


def lanes_of(shape):
    return lax.broadcasted_iota(jnp.int32, shape, 1)


def split_two(x):
    high = x.astype(BF16).astype(F32)
    return jnp.concatenate([high, x - high], axis=0).astype(BF16)


def gather_lanes(row, index):
    table = jnp.broadcast_to(row, index.shape)
    return jnp.take_along_axis(table, index, axis=1, mode="promise_in_bounds")


def one_hot_rows(index, height):
    ids = rows_of((height, LANES))
    parts = [
        jnp.where(ids == index[i : i + 1, :], 1.0, 0.0).astype(BF16) for i in range(index.shape[0])
    ]
    return jnp.concatenate(parts, axis=1)


def local_kernel(
    n, owned, count_ref, brand_ref, list_ref, slot_ref, cat_ref, meas_ref, msg_ref, table, acc
):
    step = pl.program_id(0)
    kinds, weeks, block = meas_ref.shape
    rows = kinds * weeks
    table_rows = slot_ref.shape[0]
    half = table_rows // 2
    highs = n * CAP // LOW
    chunks = block // LANES

    @pl.when(step == 0)
    def _():
        listed = list_ref[...]
        ids = rows_of((table_rows, LANES))
        lane = lanes_of((table_rows, LANES))
        low_parts, high_parts = [], []
        for i in range(n):
            same = ids == (listed[i : i + 1, :] >> 7)
            position = i * CAP + lane
            low_parts.append(jnp.where(same, (position & 255).astype(F32), 0.0).astype(BF16))
            high_parts.append(jnp.where(same, (position >> 8).astype(F32), 0.0).astype(BF16))
        left = jnp.concatenate(
            [jnp.concatenate(low_parts, axis=1), jnp.concatenate(high_parts, axis=1)], axis=0
        )
        both = dot_nt(left, one_hot_rows(listed & 127, LANES))
        positions = (both[:table_rows] + 256.0 * both[table_rows:]).astype(jnp.int32)
        table[...] = positions[:half] | (positions[half:] << 16)
        acc[...] = jnp.zeros_like(acc)

    brands = brand_ref[...]
    high_bits, low_bits = brands >> 7, brands & 127
    group = high_bits & (half - 1)
    found = jnp.zeros_like(brands)
    for q in range(half):
        found = jnp.where(group == q, gather_lanes(table[q : q + 1, :], low_bits), found)
    position = jnp.where(high_bits >= half, found >> 16, found & 0xFFFF)
    slot = step * block + rows_of(brands.shape) * LANES + lanes_of(brands.shape)
    position = jnp.where(slot < count_ref[0], position, -1)
    low, high = position & (LOW - 1), position >> 8

    values = split_two(jnp.concatenate([meas_ref[k] for k in range(kinds)], axis=0))
    masked = []
    for i in range(chunks):
        part = values[:, i * LANES : (i + 1) * LANES]
        pieces = []
        for h in range(highs):
            mask = jnp.where(high[i : i + 1, :] == h, 1.0, 0.0)
            mask = jnp.broadcast_to(mask, part.shape).astype(BF16)
            pieces.append(part * mask)
        masked.append(jnp.concatenate(pieces, axis=0))
    acc[...] += dot_nt(jnp.concatenate(masked, axis=1), one_hot_rows(low, LOW))

    @pl.when(step == pl.num_programs(0) - 1)
    def _():
        sums = []
        for h in range(highs):
            at = h * 2 * rows
            sums.append(acc[at : at + rows] + acc[at + rows : at + 2 * rows])
        sums = jnp.concatenate(sums, axis=1)
        listed = list_ref[...]
        high_bits, low_bits = listed >> 7, listed & 127
        columns = jnp.zeros_like(listed)
        cats = jnp.zeros_like(listed)
        for q in range(table_rows):
            here = high_bits == q
            columns = jnp.where(here, gather_lanes(slot_ref[q : q + 1, :], low_bits), columns)
            cats = jnp.where(here, gather_lanes(cat_ref[q : q + 1, :], low_bits), cats)
        by_cat = dot_nt(split_two(sums), one_hot_rows(cats, CAT_PAD))
        by_cat = by_cat[:rows] + by_cat[rows:]
        me = lax.axis_index("wide")
        share = table_rows // n
        my_cats = cat_ref[pl.ds(pl.multiple_of(me * share, share), share), :]
        sizes = dot_nt(jnp.ones((8, share * LANES), BF16), one_hot_rows(my_cats, CAT_PAD))
        per_row = jnp.sum(sums, axis=1, keepdims=True)
        columns = lax.rem(columns, owned).astype(F32)
        cats = cats.astype(F32)
        ids = rows_of((8, LANES))
        notes = jnp.where(ids == 2, 1.0, 0.0)
        for k in range(kinds):
            inside = (rows_of((rows, 1)) // weeks) == k
            total = jnp.sum(jnp.where(inside, per_row, 0.0), axis=0, keepdims=True)
            notes = jnp.where(ids == 3 + k, jnp.broadcast_to(total, (8, LANES)), notes)
        for w in range(n):
            at = (w // (n // CAT_BLOCKS)) * LANES
            msg_ref[w, :rows, :] = sums[:, w * LANES : (w + 1) * LANES]
            msg_ref[w, rows : rows + 8, :] = jnp.where(
                ids == 0, columns[w : w + 1, :], jnp.where(ids == 1, cats[w : w + 1, :], notes)
            )
            msg_ref[w, rows + 8 : 2 * rows + 8, :] = by_cat[:, at : at + LANES]
            msg_ref[w, 2 * rows + 8 :, :] = sizes[:, at : at + LANES]


def share_kernel(
    n, m, kinds, weeks, msg_ref, brand_ref, category_ref,
    arrived, blocks, total, totals, send1, recv1, send2, recv2, send3, recv3,
):
    rows = kinds * weeks
    owned = brand_ref.shape[2]
    me, z = lax.axis_index("wide"), lax.axis_index("narrow")
    group = n // CAT_BLOCKS
    block, sub = me // group, lax.rem(me, group)

    barrier = pltpu.get_barrier_semaphore()
    for d in range(1, n):
        pl.semaphore_signal(
            barrier, inc=1, device_id=(lax.rem(me + d, n), z), device_id_type=MESH
        )
    for e in range(1, m):
        pl.semaphore_signal(
            barrier, inc=1, device_id=(me, lax.rem(z + e, m)), device_id_type=MESH
        )
    pl.semaphore_wait(barrier, n + m - 2)

    first = []
    for d in range(1, n):
        peer = lax.rem(me + d, n)
        copy = pltpu.make_async_remote_copy(
            src_ref=msg_ref.at[peer],
            dst_ref=arrived.at[d],
            send_sem=send1.at[d],
            recv_sem=recv1.at[d],
            device_id=(peer, z),
            device_id_type=MESH,
        )
        copy.start()
        first.append(copy)
    arrived[0] = msg_ref[me]
    for copy in first:
        copy.wait()

    split = rows + 8
    reduced = arrived[0, split:, :]
    notes = arrived[0, rows:split, :]
    for d in range(1, n):
        reduced = reduced + arrived[d, split:, :]
        notes = notes + arrived[d, rows:split, :]
    blocks[block] = reduced
    total[...] = notes
    second = []
    for e in range(1, CAT_BLOCKS):
        peer = lax.rem(block + e, CAT_BLOCKS) * group + sub
        copy = pltpu.make_async_remote_copy(
            src_ref=blocks.at[block],
            dst_ref=blocks.at[block],
            send_sem=send2.at[e],
            recv_sem=recv2.at[e],
            device_id=(peer, z),
            device_id_type=MESH,
        )
        copy.start()
        second.append(copy)
    for e in range(1, m):
        copy = pltpu.make_async_remote_copy(
            src_ref=total,
            dst_ref=totals.at[e],
            send_sem=send3.at[e],
            recv_sem=recv3.at[e],
            device_id=(me, lax.rem(z + e, m)),
            device_id_type=MESH,
        )
        copy.start()
        second.append(copy)

    entries = jnp.concatenate([arrived[d, :split, :] for d in range(n)], axis=1)
    ids = rows_of((owned, LANES)).astype(F32)
    placing = jnp.concatenate(
        [
            jnp.where(ids == arrived[d, rows : rows + 1, :], 1.0, 0.0).astype(BF16)
            for d in range(n)
        ],
        axis=1,
    )
    placed = dot_nt(split_two(entries), placing)
    placed = placed[:split] + placed[split:]
    my_cat = placed[rows + 1 : rows + 2, :] / placed[rows + 2 : rows + 3, :]
    cat_ids = rows_of((CAT_PAD, owned)).astype(F32)
    member = jnp.where(jnp.abs(my_cat - cat_ids) < 0.5, 1.0, 0.0).astype(BF16)

    for copy in second:
        copy.wait()
    every = jnp.concatenate([blocks[j] for j in range(CAT_BLOCKS)], axis=1)
    sums, sizes = every[:rows], every[rows : rows + 1]
    ratio = jnp.where(sums > 0.0, sizes / sums, 0.0)
    spread = jnp.dot(split_two(ratio), member, preferred_element_type=F32)
    relative = placed[:rows] * (spread[:rows] + spread[rows:])
    grand = total[...]
    for e in range(1, m):
        grand = grand + totals[e]
    for k in range(kinds):
        at = k * weeks
        brand_ref[k] = relative[at : at + weeks]
        scale = (CATS * weeks * m) / grand[3 + k : 4 + k, :1]
        category_ref[k] = (sums[at : at + weeks] * scale)[:, :CATS]


def body(n, m, measures, sku_brand, sku_count, brand_slot, brand_category):
    kinds, weeks, tile = measures.shape
    brand_total = brand_slot.shape[0]
    owned = brand_total // n
    rows = kinds * weeks
    table_rows = brand_total // LANES
    block = min(4096, tile)
    height = 2 * rows + 16
    brands = sku_brand.reshape(-1, LANES)
    whole = lambda shape: pl.BlockSpec(shape, lambda s: (0,) * len(shape))
    msg = pl.pallas_call(
        functools.partial(local_kernel, n, owned),
        grid=(tile // block,),
        out_shape=jax.ShapeDtypeStruct((n, height, LANES), F32),
        in_specs=[
            pl.BlockSpec(memory_space=pltpu.SMEM),
            pl.BlockSpec((block // LANES, LANES), lambda s: (s, 0)),
            whole((n, LANES)),
            whole((table_rows, LANES)),
            whole((table_rows, LANES)),
            pl.BlockSpec((kinds, weeks, block), lambda s: (0, 0, s)),
        ],
        out_specs=whole((n, height, LANES)),
        scratch_shapes=[
            pltpu.VMEM((table_rows // 2, LANES), jnp.int32),
            pltpu.VMEM((n * CAP // LOW * 2 * rows, LOW), F32),
        ],
        compiler_params=pltpu.CompilerParams(dimension_semantics=("arbitrary",)),
        name="tile_sums",
    )(
        sku_count,
        brands,
        brands,
        brand_slot.reshape(-1, LANES),
        brand_category.reshape(-1, LANES),
        measures,
    )
    dma = pltpu.SemaphoreType.DMA
    return pl.pallas_call(
        functools.partial(share_kernel, n, m, kinds, weeks),
        out_shape=(
            jax.ShapeDtypeStruct((kinds, weeks, owned), F32),
            jax.ShapeDtypeStruct((kinds, weeks, CATS), F32),
        ),
        in_specs=[pl.BlockSpec(memory_space=pltpu.VMEM)],
        out_specs=(
            pl.BlockSpec(memory_space=pltpu.VMEM),
            pl.BlockSpec(memory_space=pltpu.VMEM),
        ),
        scratch_shapes=[
            pltpu.VMEM((n, height, LANES), F32),
            pltpu.VMEM((CAT_BLOCKS, rows + 8, LANES), F32),
            pltpu.VMEM((8, LANES), F32),
            pltpu.VMEM((m, 8, LANES), F32),
            dma((n,)),
            dma((n,)),
            dma((CAT_BLOCKS,)),
            dma((CAT_BLOCKS,)),
            dma((m,)),
            dma((m,)),
        ],
        compiler_params=pltpu.CompilerParams(collective_id=0, has_side_effects=True),
        name="share_sums",
    )(msg)


def solution(mesh):
    n, m = mesh.shape["wide"], mesh.shape["narrow"]
    return jax.shard_map(
        functools.partial(body, n, m),
        mesh=mesh,
        in_specs=(P(None, "narrow", "wide"), P("wide"), P("wide"), P(), P()),
        out_specs=(P(None, "narrow", "wide"), P(None, "narrow", None)),
        check_vma=False,
    )
```

time: 161 us -> 36.9 us (0.23)
  starting transfers between devices: 61.3 us -> 0 us
  blocking collectives: 34.7 us -> 0 us
  Pallas kernels: 0 us -> 26.4 us
  other arithmetic: 21.2 us -> 0 us
  local copies, waits for them, and re-layouts: 24.2 us -> 8.77 us
  matrix products: 12.4 us -> 0 us
  waiting for transfers between devices: 4.08 us -> 0 us
    all_to_all x2 -> x0, starting transfers between devices: 61.3 us -> none  [the longest x1 56.1 us: body(): lax.all_to_all(packed, 'wide', split_axis=0, concat_axis=0, tiled=True)]
    psum x2 -> x0, blocking collectives: 34.7 us -> none  [the longest x1 22.8 us: body(): category_sums = lax.psum(category_part, 'wide')]
    pallas_call x0 -> x2, Pallas kernels: none -> 26.4 us  [the longest x1 15.3 us: body(): pl.pallas_call(functools.partial(share_kernel, n, m, kinds, weeks), out_s...]
    dynamic_slice x19 -> x0, local copies, waits for them, and re-layouts: 13.1 us -> none  [the longest x8 5.54 us: lookup(): lax.dynamic_slice_in_dim(brand_category, offset, brand_block, 0)]
    dot_general x7 -> x0, matrix products: 12.4 us -> none  [the longest x3 7.87 us: accumulate(): jnp.dot(values, member_table, preferred_element_type=jnp.float32)]
    reduce_sum x18 -> x0, other arithmetic: 12 us -> none  [the longest x8 9.44 us: lookup(): jnp.sum(jnp.where(own_columns[:, None] == block_slots[None, :], block_cat...]
    all_to_all x2 -> x0, waiting for transfers between devices: 4.08 us -> none  [the longest x1 4.08 us: body(): lax.all_to_all(packed, 'wide', split_axis=0, concat_axis=0, tiled=True)]
    concatenate x1 -> x0, other arithmetic: 3.9 us -> none  [body(): stacked = jnp.concatenate([high_part, middle_part, low_part], axis=0)]
  transfers between devices with their start and end apart: 2 -> 0, of which waited for: 1 -> 0; matrix products, arithmetic and copies ran while one was open for 18% -> 0% of each run, Pallas kernels for 0% -> 0%
where the time goes in v1:
time: 36.9 us; the launch traced here: 36.5 us
  Pallas kernels  26.4 us (72%)
  local copies, waits for them, and re-layouts  8.77 us (24%)
  between operations  1.29 us (3%)
    pallas_call x1, Pallas kernels, body(): pl.pallas_call(functools.partial(share_kernel, n, m, kinds, weeks), out_s...  15.3 us
    pallas_call x1, Pallas kernels, body(): pl.pallas_call(functools.partial(local_kernel, n, owned), grid=(tile // b...  11.1 us
    unnamed x1, local copies, waits for them, and re-layouts  5.65 us
    pallas_call x2, local copies, waits for them, and re-layouts, body(): pl.pallas_call(functools.partial(share_kernel, n, m, kinds, weeks), out_s...  3.12 us

profile of v1, /device:TPU:0, one launch (start us, length us, event | category | flops | bytes accessed | tf_op | source)
XLA Modules:
  0.0 36.5 jit_solution(1159643159731247497)
XLA Ops:
  1.3 5.7 %copy.7.meas_ref = f32[2,12,32768]{2,1,0:T(8,128)} copy(f32[2,12,32768]{2,0,1:T(2,128)} %param.5) | data formatting | bytes 6291456 | tf_op args[0]
  6.9 11.1 %tile_sums.1.msg_ref = f32[8,64,128]{2,1,0:T(8,128)} custom-call(s32[1]{0:T(128)S(6)} %copy.10.count_ref, s32[256,128]{1,0:T(8,128)} %bitcast.3, s32[256,128]{1,0:T(8,128)} %bitcast.4, s32[64,128]{1,0:T(8,128)} %bitcast.5, s32[64,128]{1,0:T(8,128)} %bitcast.6, f32[2,12,32768]{2,1,0:T(8,128)} %copy.7.meas_ref), custom_call_target="tpu_custom_call" | custom-call | tf_op jit(solution)/shard_map/tile_sums/pallas_call | solution.py:258
  18.0 15.3 %share_sums.1 = (f32[2,12,1024]{2,1,0:T(8,128)}, f32[2,12,500]{2,1,0:T(8,128)}) custom-call(f32[8,64,128]{2,1,0:T(8,128)} %tile_sums.1.msg_ref), custom_call_target="tpu_custom_call" | custom-call | tf_op jit(solution)/shard_map/share_sums/pallas_call | solution.py:286
  33.3 1.6 %copy.8 = f32[2,12,1024]{2,0,1:T(2,128)} copy(f32[2,12,1024]{2,1,0:T(8,128)} %get-tuple-element.2) | data formatting | bytes 196608 | tf_op jit(solution)/shard_map/share_sums/pallas_call | solution.py:286
  35.0 1.5 %copy.9 = f32[2,12,500]{2,0,1:T(2,128)} copy(f32[2,12,500]{2,1,0:T(8,128)} %get-tuple-element.3) | data formatting | bytes 96000 | tf_op jit(solution)/shard_map/share_sums/pallas_call | solution.py:286

commit v2 on v1

v2 whole, which is shorter than its diff:
```python
import functools

import jax
import jax.numpy as jnp
from jax import lax
from jax.experimental import pallas as pl
from jax.experimental.pallas import tpu as pltpu
from jax.sharding import PartitionSpec as P

CATS = 500
CAP = 128
LANES = 128
CAT_BLOCKS = 4
CAT_PAD = CAT_BLOCKS * LANES
NT = (((1,), (1,)), ((), ()))
MESH = pl.DeviceIdType.MESH
F32 = jnp.float32
BF16 = jnp.bfloat16


def dot_nt(a, b):
    return lax.dot_general(a, b, NT, preferred_element_type=F32)


def rows_of(shape):
    return lax.broadcasted_iota(jnp.int32, shape, 0)


def lanes_of(shape):
    return lax.broadcasted_iota(jnp.int32, shape, 1)


def split_two(x):
    high = x.astype(BF16).astype(F32)
    return jnp.concatenate([high, x - high], axis=0).astype(BF16)


def gather_lanes(row, index):
    table = jnp.broadcast_to(row, index.shape)
    return jnp.take_along_axis(table, index, axis=1, mode="promise_in_bounds")


def one_hot_rows(index, height):
    ids = rows_of((height, LANES))
    parts = [
        jnp.where(ids == index[i : i + 1, :], 1.0, 0.0).astype(BF16) for i in range(index.shape[0])
    ]
    return jnp.concatenate(parts, axis=1)


def packed_row(row):
    return jnp.broadcast_to(row.astype(F32), (16, LANES)).astype(BF16)


def load_block(meas_ref, values, arrivals, step, per_block, start):
    weeks, _, kinds, _ = meas_ref.shape
    chunks = pl.ds(step * per_block, per_block)
    for w in range(weeks):
        copy = pltpu.make_async_copy(
            meas_ref.at[w, chunks],
            values.at[chunks, pl.ds(kinds * w, kinds)],
            arrivals.at[step, w],
        )
        if start:
            copy.start()
        else:
            copy.wait()


def local_sums(n, owned, count_ref, brand_ref, slot_ref, cat_ref, meas_ref, msg_ref, values, table, places, acc, arrivals):
    rows = values.shape[1]
    kinds = meas_ref.shape[2]
    table_rows = slot_ref.shape[0]
    half = table_rows // 2
    steps = arrivals.shape[0]
    per_block = values.shape[0] // steps

    listed = brand_ref[:n, :]
    ids = rows_of((table_rows, LANES))
    lane = lanes_of((table_rows, LANES))
    low_parts, high_parts = [], []
    for i in range(n):
        same = ids == (listed[i : i + 1, :] >> 7)
        low_parts.append(jnp.where(same, lane.astype(F32), 0.0).astype(BF16))
        high_parts.append(jnp.where(same, float(i), 0.0).astype(BF16))
    left = jnp.concatenate(
        [jnp.concatenate(low_parts, axis=1), jnp.concatenate(high_parts, axis=1)], axis=0
    )
    both = dot_nt(left, one_hot_rows(listed & 127, LANES))
    positions = (both[:table_rows] + float(CAP) * both[table_rows:]).astype(jnp.int32)
    table[...] = positions[:half] | (positions[half:] << 16)
    acc[...] = jnp.zeros_like(acc)

    def find(step, carry):
        here = pl.ds(pl.multiple_of(step * per_block, per_block), per_block)
        brands = brand_ref[here, :]
        high_bits, low_bits = brands >> 7, brands & 127
        group = high_bits & (half - 1)
        found = jnp.zeros_like(brands)
        for q in range(half):
            found = jnp.where(group == q, gather_lanes(table[q : q + 1, :], low_bits), found)
        position = jnp.where(high_bits >= half, found >> 16, found & 0xFFFF)
        slot = (step * per_block + rows_of(brands.shape)) * LANES + lanes_of(brands.shape)
        places[here, :] = jnp.where(slot < count_ref[0], position, -1)
        return carry

    lax.fori_loop(0, steps, find, 0)

    high_bits, low_bits = listed >> 7, listed & 127
    columns = jnp.zeros_like(listed)
    cats = jnp.zeros_like(listed)
    for q in range(table_rows):
        here = high_bits == q
        columns = jnp.where(here, gather_lanes(slot_ref[q : q + 1, :], low_bits), columns)
        cats = jnp.where(here, gather_lanes(cat_ref[q : q + 1, :], low_bits), cats)
    me = lax.axis_index("wide")
    share = table_rows // n
    my_cats = cat_ref[pl.ds(pl.multiple_of(me * share, share), share), :]
    sizes = dot_nt(jnp.ones((8, share * LANES), BF16), one_hot_rows(my_cats, CAT_PAD))
    by_list = one_hot_rows(cats, CAT_PAD)

    lane_ids = rows_of((LANES, LANES)).astype(F32).astype(BF16).reshape(LANES // 16, 16, LANES)
    one, zero = jnp.ones((), BF16), jnp.zeros((), BF16)

    def add(step, carry):
        load_block(meas_ref, values, arrivals, step, per_block, False)
        here = pl.multiple_of(step * per_block, per_block)
        position = places[pl.ds(here, per_block), :]
        low, high = position & (CAP - 1), position >> 7
        masked, hot = [], []
        for i in range(per_block):
            part = split_two(values[here + i]).reshape(2 * rows // 16, 16, LANES)
            owner = packed_row(high[i : i + 1, :])
            pieces = [
                jnp.where((owner == float(h))[None], part, zero).reshape(2 * rows, LANES)
                for h in range(n)
            ]
            masked.append(jnp.concatenate(pieces, axis=0))
            match = lane_ids == packed_row(low[i : i + 1, :])[None]
            hot.append(jnp.where(match, one, zero).reshape(LANES, LANES))
        acc[...] += dot_nt(jnp.concatenate(masked, axis=1), jnp.concatenate(hot, axis=1))
        return carry

    lax.fori_loop(0, steps, add, 0)

    sums = []
    for h in range(n):
        at = h * 2 * rows
        sums.append(acc[at : at + rows] + acc[at + rows : at + 2 * rows])
    sums = jnp.concatenate(sums, axis=1)
    by_cat = dot_nt(split_two(sums), by_list)
    by_cat = by_cat[:rows] + by_cat[rows:]
    per_row = jnp.sum(sums, axis=1, keepdims=True)
    columns = lax.rem(columns, owned).astype(F32)
    cats = cats.astype(F32)
    ids = rows_of((8, LANES))
    notes = jnp.where(ids == 2, 1.0, 0.0)
    for k in range(kinds):
        inside = lax.rem(rows_of((rows, 1)), kinds) == k
        total = jnp.sum(jnp.where(inside, per_row, 0.0), axis=0, keepdims=True)
        notes = jnp.where(ids == 3 + k, jnp.broadcast_to(total, (8, LANES)), notes)
    for w in range(n):
        at = (w // (n // CAT_BLOCKS)) * LANES
        msg_ref[w, 0, :rows, :] = by_cat[:, at : at + LANES]
        msg_ref[w, 0, rows:, :] = jnp.where(
            ids == 0, sizes[:, at : at + LANES], notes
        )
        msg_ref[w, 1, :rows, :] = sums[:, w * LANES : (w + 1) * LANES]
        msg_ref[w, 1, rows:, :] = jnp.where(
            ids == 0, columns[w : w + 1, :], jnp.where(ids == 1, cats[w : w + 1, :], notes)
        )


def rollup_kernel(
    n, m, owned, count_ref, brand_list_ref, slot_ref, cat_ref, meas_ref, brand_ref, category_ref,
    msg_ref, values, table, places, acc, arrivals,
    arrived, blocks, total, totals, send1, recv1, send2, recv2, send3, recv3,
):
    weeks, chunks, kinds, _ = meas_ref.shape
    rows = kinds * weeks
    steps = arrivals.shape[0]
    me, z = lax.axis_index("wide"), lax.axis_index("narrow")
    group = n // CAT_BLOCKS
    block, sub = me // group, lax.rem(me, group)

    barrier = pltpu.get_barrier_semaphore()
    for d in range(1, n):
        pl.semaphore_signal(
            barrier, inc=1, device_id=(lax.rem(me + d, n), z), device_id_type=MESH
        )
    for e in range(1, m):
        pl.semaphore_signal(
            barrier, inc=1, device_id=(me, lax.rem(z + e, m)), device_id_type=MESH
        )
    for step in range(steps):
        load_block(meas_ref, values, arrivals, step, chunks // steps, True)
    local_sums(
        n, owned, count_ref, brand_list_ref, slot_ref, cat_ref, meas_ref,
        msg_ref, values, table, places, acc, arrivals,
    )
    pl.semaphore_wait(barrier, n + m - 2)

    first = ([], [])
    for part in range(2):
        for d in range(1, n):
            peer = lax.rem(me + d, n)
            copy = pltpu.make_async_remote_copy(
                src_ref=msg_ref.at[peer, part],
                dst_ref=arrived.at[d, part],
                send_sem=send1.at[d, part],
                recv_sem=recv1.at[d, part],
                device_id=(peer, z),
                device_id_type=MESH,
            )
            copy.start()
            first[part].append(copy)
    reduced = msg_ref[me, 0]
    arrived[0, 1] = msg_ref[me, 1]
    for d in range(1, n):
        first[0][d - 1].wait()
        reduced = reduced + arrived[d, 0]
    blocks[block] = reduced
    total[...] = reduced[rows:]
    second = []
    for e in range(1, CAT_BLOCKS):
        peer = lax.rem(block + e, CAT_BLOCKS) * group + sub
        copy = pltpu.make_async_remote_copy(
            src_ref=blocks.at[block],
            dst_ref=blocks.at[block],
            send_sem=send2.at[e],
            recv_sem=recv2.at[e],
            device_id=(peer, z),
            device_id_type=MESH,
        )
        copy.start()
        second.append(copy)
    for e in range(1, m):
        copy = pltpu.make_async_remote_copy(
            src_ref=total,
            dst_ref=totals.at[e],
            send_sem=send3.at[e],
            recv_sem=recv3.at[e],
            device_id=(me, lax.rem(z + e, m)),
            device_id_type=MESH,
        )
        copy.start()
        second.append(copy)

    for copy in first[1]:
        copy.wait()
    split = rows + 8
    entries = jnp.concatenate([arrived[d, 1] for d in range(n)], axis=1)
    ids = rows_of((owned, LANES)).astype(F32)
    placing = jnp.concatenate(
        [
            jnp.where(ids == arrived[d, 1, rows : rows + 1, :], 1.0, 0.0).astype(BF16)
            for d in range(n)
        ],
        axis=1,
    )
    placed = dot_nt(split_two(entries), placing)
    placed = placed[:split] + placed[split:]
    my_cat = placed[rows + 1 : rows + 2, :] / placed[rows + 2 : rows + 3, :]
    cat_ids = rows_of((CAT_PAD, owned)).astype(F32)
    member = jnp.where(jnp.abs(my_cat - cat_ids) < 0.5, 1.0, 0.0).astype(BF16)

    for copy in second:
        copy.wait()
    every = jnp.concatenate([blocks[j] for j in range(CAT_BLOCKS)], axis=1)
    sums, sizes = every[:rows], every[rows : rows + 1]
    ratio = jnp.where(sums > 0.0, sizes / sums, 0.0)
    spread = jnp.dot(split_two(ratio), member, preferred_element_type=F32)
    relative = placed[:rows] * (spread[:rows] + spread[rows:])
    grand = total[...]
    for e in range(1, m):
        grand = grand + totals[e]
    scale = (CATS * weeks * m) / grand
    odd = lax.rem(rows_of((rows, 1)), kinds)
    row_scale = jnp.zeros((rows, 1), F32)
    for k in range(kinds):
        row_scale = jnp.where(odd == k, scale[3 + k : 4 + k, :1], row_scale)
    indices = sums * row_scale
    for w in range(weeks):
        at = kinds * w
        for c in range(owned // LANES):
            brand_ref[w, kinds * c : kinds * (c + 1), :] = relative[
                at : at + kinds, c * LANES : (c + 1) * LANES
            ]
        for c in range(CAT_BLOCKS):
            category_ref[w, kinds * c : kinds * (c + 1), :] = indices[
                at : at + kinds, c * LANES : (c + 1) * LANES
            ]


def body(n, m, measures, sku_brand, sku_count, brand_slot, brand_category):
    kinds, weeks, tile = measures.shape
    brand_total = brand_slot.shape[0]
    owned = brand_total // n
    rows = kinds * weeks
    table_rows = brand_total // LANES
    chunks = tile // LANES
    steps = chunks // 32
    by_chunk = measures.reshape(kinds, weeks, chunks, LANES).transpose(1, 2, 0, 3)
    dma = pltpu.SemaphoreType.DMA
    vmem = pl.BlockSpec(memory_space=pltpu.VMEM)
    brand_out, category_out = pl.pallas_call(
        functools.partial(rollup_kernel, n, m, owned),
        out_shape=(
            jax.ShapeDtypeStruct((weeks, kinds * owned // LANES, LANES), F32),
            jax.ShapeDtypeStruct((weeks, kinds * CAT_BLOCKS, LANES), F32),
        ),
        in_specs=[
            pl.BlockSpec(memory_space=pltpu.SMEM),
            vmem,
            vmem,
            vmem,
            pl.BlockSpec(memory_space=pl.ANY),
        ],
        out_specs=(vmem, vmem),
        scratch_shapes=[
            pltpu.VMEM((n, 2, rows + 8, LANES), F32),
            pltpu.VMEM((chunks, rows, LANES), F32),
            pltpu.VMEM((table_rows // 2, LANES), jnp.int32),
            pltpu.VMEM((chunks, LANES), jnp.int32),
            pltpu.VMEM((n * 2 * rows, LANES), F32),
            dma((steps, weeks)),
            pltpu.VMEM((n, 2, rows + 8, LANES), F32),
            pltpu.VMEM((CAT_BLOCKS, rows + 8, LANES), F32),
            pltpu.VMEM((8, LANES), F32),
            pltpu.VMEM((m, 8, LANES), F32),
            dma((n, 2)),
            dma((n, 2)),
            dma((CAT_BLOCKS,)),
            dma((CAT_BLOCKS,)),
            dma((m,)),
            dma((m,)),
        ],
        compiler_params=pltpu.CompilerParams(collective_id=0, has_side_effects=True),
        name="rollup",
    )(
        sku_count,
        sku_brand.reshape(-1, LANES),
        brand_slot.reshape(-1, LANES),
        brand_category.reshape(-1, LANES),
        by_chunk,
    )
    brand_index = brand_out.reshape(weeks, -1, kinds, LANES).transpose(2, 0, 1, 3)
    category_index = category_out.reshape(weeks, -1, kinds, LANES).transpose(2, 0, 1, 3)
    return (
        brand_index.reshape(kinds, weeks, owned),
        category_index.reshape(kinds, weeks, CAT_PAD)[:, :, :CATS],
    )


def solution(mesh):
    n, m = mesh.shape["wide"], mesh.shape["narrow"]
    return jax.shard_map(
        functools.partial(body, n, m),
        mesh=mesh,
        in_specs=(P(None, "narrow", "wide"), P("wide"), P("wide"), P(), P()),
        out_specs=(P(None, "narrow", "wide"), P(None, "narrow", None)),
        check_vma=False,
    )
```

time: 36.9 us -> 31.7 us (0.86)
  local copies, waits for them, and re-layouts: 8.77 us -> 2.96 us
  Pallas kernels: 26.4 us -> 27.2 us
    pallas_call x2 -> x0, local copies, waits for them, and re-layouts: 3.12 us -> none  [body(): pl.pallas_call(functools.partial(share_kernel, n, m, kinds, weeks), out_s...]
    unnamed x1 -> x2, local copies, waits for them, and re-layouts: 5.65 us -> 2.96 us
    pallas_call x2 -> x1, Pallas kernels: 26.4 us -> 27.2 us  [body(): pl.pallas_call(functools.partial(rollup_kernel, n, m, owned), out_shape=(...]
where the time goes in v2:
time: 31.7 us; the launch traced here: 31.5 us
  Pallas kernels  27.2 us (86%)
  local copies, waits for them, and re-layouts  2.96 us (9%)
  between operations  1.28 us (4%)
    pallas_call x1, Pallas kernels, body(): pl.pallas_call(functools.partial(rollup_kernel, n, m, owned), out_shape=(...  27.2 us
    unnamed x2, local copies, waits for them, and re-layouts  2.96 us

profile of v2, /device:TPU:0, one launch (start us, length us, event | category | flops | bytes accessed | tf_op | source)
XLA Modules:
  0.0 31.5 jit_solution(16420964927243252036)
XLA Ops:
  1.3 27.2 %rollup.1 = (f32[12,16,128]{2,1,0:T(8,128)}, f32[12,8,128]{2,1,0:T(8,128)}) custom-call(s32[1]{0:T(128)S(6)} %copy.11.count_ref, s32[256,128]{1,0:T(8,128)} %bitcast.18, s32[64,128]{1,0:T(8,128)} %bitcast.21, s32[64,128]{1,0:T(8,128)} %bitcast.22, f32[12,256,2,128]{3,2,1,0:T(2,128)} %bitcast.17), custom_call_target="tpu_custom_call" | custom-call | tf_op jit(solution)/shard_map/rollup/pallas_call | solution.py:306
  28.5 1.5 %copy.12 = f32[2,12,1024]{2,0,1:T(2,128)} copy(f32[2,12,1024]{2,0,1:T(2,128)} %bitcast.19) | data formatting | bytes 196608
  30.1 1.4 %copy.13 = f32[2,12,500]{2,0,1:T(2,128)} copy(f32[2,12,500]{2,0,1:T(2,128)} %bitcast.20) | data formatting | bytes 96000

commit v3 on v2

--- a/solution.py
+++ b/solution.py
@@ -10,6 +10,7 @@
 CATS = 500
 CAP = 128
 LANES = 128
+LOW = 256
 CAT_BLOCKS = 4
 CAT_PAD = CAT_BLOCKS * LANES
 NT = (((1,), (1,)), ((), ()))
@@ -40,16 +41,24 @@
     return jnp.take_along_axis(table, index, axis=1, mode="promise_in_bounds")
 
 
-def one_hot_rows(index, height):
-    ids = rows_of((height, LANES))
-    parts = [
-        jnp.where(ids == index[i : i + 1, :], 1.0, 0.0).astype(BF16) for i in range(index.shape[0])
-    ]
-    return jnp.concatenate(parts, axis=1)
-
-
 def packed_row(row):
     return jnp.broadcast_to(row.astype(F32), (16, LANES)).astype(BF16)
+
+
+def one_hot_row(row, height):
+    span = min(height, 256)
+    ids = rows_of((span, LANES)).astype(F32).astype(BF16).reshape(span // 16, 16, LANES)
+    one, zero = jnp.ones((), BF16), jnp.zeros((), BF16)
+    parts = [
+        jnp.where(ids == packed_row(row - base)[None], one, zero).reshape(span, LANES)
+        for base in range(0, height, span)
+    ]
+    return jnp.concatenate(parts, axis=0)
+
+
+def one_hot_rows(index, height):
+    parts = [one_hot_row(index[i : i + 1, :], height) for i in range(index.shape[0])]
+    return jnp.concatenate(parts, axis=1)
 
 
 def load_block(meas_ref, values, arrivals, step, per_block, start):
@@ -119,32 +128,42 @@
     sizes = dot_nt(jnp.ones((8, share * LANES), BF16), one_hot_rows(my_cats, CAT_PAD))
     by_list = one_hot_rows(cats, CAT_PAD)
 
-    lane_ids = rows_of((LANES, LANES)).astype(F32).astype(BF16).reshape(LANES // 16, 16, LANES)
+    highs = n * CAP // LOW
+    lane_ids = [
+        (lanes_of((LANES, LANES)) + at).astype(F32).astype(BF16) for at in range(0, LOW, LANES)
+    ]
     one, zero = jnp.ones((), BF16), jnp.zeros((), BF16)
 
     def add(step, carry):
         load_block(meas_ref, values, arrivals, step, per_block, False)
         here = pl.multiple_of(step * per_block, per_block)
         position = places[pl.ds(here, per_block), :]
-        low, high = position & (CAP - 1), position >> 7
+        low, high = position & (LOW - 1), position >> (LOW.bit_length() - 1)
+        columns_of = jnp.transpose(low.astype(F32))
         masked, hot = [], []
         for i in range(per_block):
             part = split_two(values[here + i]).reshape(2 * rows // 16, 16, LANES)
             owner = packed_row(high[i : i + 1, :])
             pieces = [
                 jnp.where((owner == float(h))[None], part, zero).reshape(2 * rows, LANES)
-                for h in range(n)
+                for h in range(highs)
             ]
             masked.append(jnp.concatenate(pieces, axis=0))
-            match = lane_ids == packed_row(low[i : i + 1, :])[None]
-            hot.append(jnp.where(match, one, zero).reshape(LANES, LANES))
-        acc[...] += dot_nt(jnp.concatenate(masked, axis=1), jnp.concatenate(hot, axis=1))
+            column = jnp.broadcast_to(columns_of[:, i : i + 1], (LANES, LANES)).astype(BF16)
+            hot.append(
+                jnp.concatenate([jnp.where(column == ids, one, zero) for ids in lane_ids], axis=1)
+            )
+        acc[...] += jnp.dot(
+            jnp.concatenate(masked, axis=1),
+            jnp.concatenate(hot, axis=0),
+            preferred_element_type=F32,
+        )
         return carry
 
     lax.fori_loop(0, steps, add, 0)
 
     sums = []
-    for h in range(n):
+    for h in range(highs):
         at = h * 2 * rows
         sums.append(acc[at : at + rows] + acc[at + rows : at + 2 * rows])
     sums = jnp.concatenate(sums, axis=1)
@@ -250,13 +269,8 @@
         copy.wait()
     split = rows + 8
     entries = jnp.concatenate([arrived[d, 1] for d in range(n)], axis=1)
-    ids = rows_of((owned, LANES)).astype(F32)
     placing = jnp.concatenate(
-        [
-            jnp.where(ids == arrived[d, 1, rows : rows + 1, :], 1.0, 0.0).astype(BF16)
-            for d in range(n)
-        ],
-        axis=1,
+        [one_hot_row(arrived[d, 1, rows : rows + 1, :], owned) for d in range(n)], axis=1
     )
     placed = dot_nt(split_two(entries), placing)
     placed = placed[:split] + placed[split:]
@@ -290,6 +304,11 @@
             category_ref[w, kinds * c : kinds * (c + 1), :] = indices[
                 at : at + kinds, c * LANES : (c + 1) * LANES
             ]
+
+
+def hand_out(brand_ref, category_ref, brand_out, category_out):
+    brand_out[...] = brand_ref[...]
+    category_out[...] = category_ref[...]
 
 
 def body(n, m, measures, sku_brand, sku_count, brand_slot, brand_category):
@@ -322,7 +341,7 @@
             pltpu.VMEM((chunks, rows, LANES), F32),
             pltpu.VMEM((table_rows // 2, LANES), jnp.int32),
             pltpu.VMEM((chunks, LANES), jnp.int32),
-            pltpu.VMEM((n * 2 * rows, LANES), F32),
+            pltpu.VMEM((n * CAP // LOW * 2 * rows, LOW), F32),
             dma((steps, weeks)),
             pltpu.VMEM((n, 2, rows + 8, LANES), F32),
             pltpu.VMEM((CAT_BLOCKS, rows + 8, LANES), F32),
@@ -344,6 +363,16 @@
         brand_category.reshape(-1, LANES),
         by_chunk,
     )
+    brand_out, category_out = pl.pallas_call(
+        hand_out,
+        out_shape=(
+            jax.ShapeDtypeStruct(brand_out.shape, F32),
+            jax.ShapeDtypeStruct(category_out.shape, F32),
+        ),
+        in_specs=[vmem, vmem],
+        out_specs=(vmem, vmem),
+        name="hand_out",
+    )(brand_out, category_out)
     brand_index = brand_out.reshape(weeks, -1, kinds, LANES).transpose(2, 0, 1, 3)
     category_index = category_out.reshape(weeks, -1, kinds, LANES).transpose(2, 0, 1, 3)
     return (

time: 31.7 us -> 29.2 us (0.921)
  local copies, waits for them, and re-layouts: 2.96 us -> 0 us
  Pallas kernels: 27.2 us -> 27.7 us
    unnamed x2 -> x0, local copies, waits for them, and re-layouts: 2.96 us -> none
    pallas_call x0 -> x1, Pallas kernels: none -> 1.56 us  [body(): pl.pallas_call(hand_out, out_shape=(jax.ShapeDtypeStruct(brand_out.shape,...]
    pallas_call x1, Pallas kernels: 27.2 us -> 26.2 us  [body(): pl.pallas_call(functools.partial(rollup_kernel, n, m, owned), out_shape=(...]
where the time goes in v3:
time: 29.2 us; the launch traced here: 29 us
  Pallas kernels  27.7 us (95%)
  between operations  1.28 us (4%)
    pallas_call x1, Pallas kernels, body(): pl.pallas_call(functools.partial(rollup_kernel, n, m, owned), out_shape=(...  26.2 us
    pallas_call x1, Pallas kernels, body(): pl.pallas_call(hand_out, out_shape=(jax.ShapeDtypeStruct(brand_out.shape,...  1.56 us

profile of v3, /device:TPU:0, one launch (start us, length us, event | category | flops | bytes accessed | tf_op | source)
XLA Modules:
  0.0 29.0 jit_solution(8456612106088995870)
XLA Ops:
  1.3 26.2 %rollup.1 = (f32[12,16,128]{2,1,0:T(8,128)}, f32[12,8,128]{2,1,0:T(8,128)}) custom-call(s32[1]{0:T(128)S(6)} %copy.9.count_ref, s32[256,128]{1,0:T(8,128)} %bitcast.18, s32[64,128]{1,0:T(8,128)} %bitcast.19, s32[64,128]{1,0:T(8,128)} %bitcast.20, f32[12,256,2,128]{3,2,1,0:T(2,128)} %bitcast.17), custom_call_target="tpu_custom_call" | custom-call | tf_op jit(solution)/shard_map/rollup/pallas_call | solution.py:325
  27.4 1.6 %hand_out.1 = (f32[12,16,128]{2,1,0:T(8,128)}, f32[12,8,128]{2,1,0:T(8,128)}) custom-call(f32[12,16,128]{2,1,0:T(8,128)} %get-tuple-element.6.brand_ref, f32[12,8,128]{2,1,0:T(8,128)} %get-tuple-element.7.category_ref), custom_call_target="tpu_custom_call" | custom-call | tf_op jit(solution)/shard_map/hand_out/pallas_call | solution.py:366
